TPU v7x, 32 devices: a whole 2x2x4 slice. The times are simulated.
32 devices in a mesh: groups: 2 (over y), blk: 4 (over z), rep: 2 (over x), sub: 2 (over core).
Axes of the slice: x: 2, y: 2, z: 4, core: 2. Of those that a mesh axis runs over, the one named last changes fastest.
Arguments:
- replica_delta: bfloat16 [32, 32, 4608], P(('groups', 'blk', 'rep', 'sub')), parts along dimension 0, may hold values from -150 to 150
- momentum: float32 [64, 4608], P(('groups', 'blk')), parts along dimension 0, may hold values from -6 to 6
- params: float32 [64, 4608], P(('groups', 'blk')), parts along dimension 0, may hold values from -6 to 6
- prev_master: float32 [64, 4608], P(('groups', 'blk')), parts along dimension 0, may hold values from -6 to 6
Outputs:
- new_params: float32 [64, 4608], P(('groups', 'blk')), parts along dimension 0
- new_momentum: float32 [64, 4608], P(('groups', 'blk')), parts along dimension 0
- prev_weights: bfloat16 [64, 4608], P('groups'), parts along dimension 0
There are 2 independent parts, one for each index of `groups`. A program takes and returns all parts, laid end to end along the dimension named above; each array names one. Nothing has to cross between parts.
All inputs are finite; a program needn't handle non-finite values.
Results may differ from a plain program's by a relative error of at most 0.012.
Values may be sent and summed in bfloat16 or wider, within the bound.
No kernel may reach another device: no remote copies, remote signals or barrier semaphores. Data moves between devices by JAX's collectives and lax.ppermute only.
A program may use at most 64 MiB of HBM per device.

v0:
```python
import jax
import jax.numpy as jnp
from jax import lax
from jax.sharding import PartitionSpec as P

momentum_coef = 0.9
outer_rate = 0.7


def per_device(replica_delta, momentum, params, prev_master):
    own_delta = replica_delta[0]
    width = own_delta.shape[1]
    entries = own_delta.shape[0] * width
    share_sum = lax.psum_scatter(
        own_delta.astype(jnp.float32).astype(jnp.bfloat16), "blk", scatter_dimension=0, tiled=True
    )
    summed = lax.psum(share_sum, ("rep", "sub")).astype(jnp.float32)
    squares = lax.psum(jnp.sum(summed * summed), "blk")
    clip_factor = jnp.minimum(
        jnp.float32(1.0), jnp.sqrt(jnp.float32(entries)) / jnp.sqrt(squares + 1e-06)
    )
    scaled = clip_factor * summed
    new_momentum = momentum_coef * momentum + scaled
    new_params = params - outer_rate * (scaled + momentum_coef * new_momentum)
    prev_weights = lax.all_gather(prev_master.astype(jnp.bfloat16), "blk", axis=0, tiled=True)
    return (new_params, new_momentum, prev_weights)


def solution(mesh):
    in_specs = (
        P(("groups", "blk", "rep", "sub"), None, None),
        P(("groups", "blk"), None),
        P(("groups", "blk"), None),
        P(("groups", "blk"), None),
    )
    out_specs = (P(("groups", "blk"), None), P(("groups", "blk"), None), P("groups", None))
    return jax.shard_map(
        per_device, mesh=mesh, in_specs=in_specs, out_specs=out_specs, check_vma=False
    )
```

profile of v0, /device:TPU:0, one launch (start us, length us, event | category | flops | bytes accessed | tf_op | source)
XLA Modules:
  0.0 86.8 jit_solution(3447558341183904942)
XLA Ops:
  7.2 0.0 reduce-scatter.2.cloned.1.call-start
  7.2 0.0 copy-start.1
  7.2 0.7 reduce-scatter.2.cloned.1.call-update
  7.9 0.0 all-reduce.2.cloned.1.call-start
  7.9 0.2 copy-done.1
  8.1 25.1 %reduce-scatter.2.cloned.1.call-done = bf16[8,4608]{1,0:T(8,128)(2,1)} async-done(((bf16[32,4608]{1,0:T(8,128)(2,1)}), bf16[8,4608]{1,0:T(8,128)(2,1)}) %reduce-scatter.2.cloned.1.call-update) | async-done | bytes 73744 | tf_op jit(solution)/shard_map/reduce_scatter | solution.py:14
  33.2 0.0 all-reduce.2.cloned.1.call-update
  33.2 0.0 copy-start.2
  33.2 0.0 copy-start.3
  33.2 14.1 %all_gather.3 = bf16[32,4608]{1,0:T(8,128)(2,1)S(1)} all-gather(bf16[8,4608]{1,0:T(8,128)(2,1)S(1)} %convert_element_type.9), channel_id=1, replica_groups=mesh['groups'=2,'blk'=4,'rep'=2,'sub'=2] {'blk'}, dimensions={0}, use_global_device_ids=true | all-gather | bytes 368640 | tf_op jit(solution)/shard_map/all_gather | solution.py:25
  47.4 16.1 %all-reduce.2.cloned.1.call-done = bf16[8,4608]{1,0:T(8,128)(2,1)} async-done(((bf16[8,4608]{1,0:T(8,128)(2,1)}), bf16[8,4608]{1,0:T(8,128)(2,1)}) %all-reduce.2.cloned.1.call-update) | async-done | bytes 73744 | tf_op jit(solution)/shard_map/psum | solution.py:17
  63.5 0.0 copy-start
  63.5 1.6 %fusion.4 = f32[]{:T(128)} fusion(bf16[8,4608]{1,0:T(8,128)(2,1)} %all-reduce.2.cloned.1.call-done), kind=kLoop, calls=%fused_computation.6 | loop fusion | flops 110591 | bytes 73732 | tf_op jit(solution)/shard_map/reduce_sum | solution.py:18
  65.1 12.7 %psum.15 = f32[]{:T(128)} all-reduce(f32[]{:T(128)} %fusion.4), channel_id=1, replica_groups=mesh['groups'=2,'blk'=4,'rep'=2,'sub'=2] {'blk'}, use_global_device_ids=true, to_apply=%region_3.0 | all-reduce | flops 1 | bytes 8 | tf_op jit(solution)/shard_map/psum | solution.py:18
  78.4 0.0 copy-done.2
  78.5 0.0 copy-done.3
  78.5 0.0 copy-done
  78.5 0.8 fusion.3
  79.2 0.7 copy.9
  (1 shorter events, 0.0 us)
Async XLA Ops:
  7.2 26.0 %reduce-scatter.2.cloned.1.call-start = ((), (), s32[]{:S(2)}) async-start(), calls=%async_computation.1 | async-start | bytes 368640 | tf_op jit(solution)/shard_map/reduce_scatter | solution.py:14
  7.2 0.9 %copy-start.1 = (f32[8,4608]{1,0:T(8,128)S(1)}, f32[8,4608]{1,0:T(8,128)}, u32[]{:S(2)}) copy-start(f32[8,4608]{1,0:T(8,128)} %param.7) | copy-start | bytes 442372
  7.9 55.6 %all-reduce.2.cloned.1.call-start = ((), (), s32[]{:S(2)}) async-start(), calls=%async_computation.2 | async-start | bytes 147456 | tf_op jit(solution)/shard_map/psum | solution.py:17
  33.2 45.2 %copy-start.2 = (f32[8,4608]{1,0:T(8,128)S(1)}, f32[8,4608]{1,0:T(8,128)}, u32[]{:S(2)}) copy-start(f32[8,4608]{1,0:T(8,128)} %param.6) | copy-start | bytes 442372
  33.2 45.2 %copy-start.3 = (f32[8,4608]{1,0:T(8,128)S(1)}, f32[8,4608]{1,0:T(8,128)}, u32[]{:S(2)}) copy-start(f32[8,4608]{1,0:T(8,128)} %param.5) | copy-start | bytes 442372
  63.5 15.0 %copy-start = (bf16[8,4608]{1,0:T(8,128)(2,1)S(1)}, bf16[8,4608]{1,0:T(8,128)(2,1)}, u32[]{:S(2)}) copy-start(bf16[8,4608]{1,0:T(8,128)(2,1)} %all-reduce.2.cloned.1.call-done) | copy-start | bytes 221188
Sparse Core Ops, SparseCore 0:
  10.2 22.9 reduce-scatter.1
  35.5 27.9 all-reduce.1
where the time goes:
time: 87 us; the launch traced here: 86.8 us
  waiting for transfers between devices  41.9 us (48%)
  blocking collectives  26.8 us (31%)
  between operations  14.8 us (17%)
  other arithmetic  2.36 us (3%)
  local copies, waits for them, and re-layouts  0.91 us (1%)
    reduce_scatter x1, waiting for transfers between devices, per_device(): lax.psum_scatter(own_delta.astype(jnp.float32).astype(jnp.bfloat16), 'blk...  25.1 us
    psum x1, waiting for transfers between devices, per_device(): summed = lax.psum(share_sum, ('rep', 'sub')).astype(jnp.float32)  16.1 us
    all_gather x1, blocking collectives, per_device(): lax.all_gather(prev_master.astype(jnp.bfloat16), 'blk', axis=0, tiled=True)  14.1 us
    psum x1, blocking collectives, per_device(): squares = lax.psum(jnp.sum(summed * summed), 'blk')  12.7 us
  transfers between devices with their start and end apart: 2, of which 2 were waited for; matrix products, arithmetic and copies ran while one was open for 0% of the time, Pallas kernels for 0%

commit v1 on v0

--- a/solution.py
+++ b/solution.py
@@ -14,7 +14,7 @@
     share_sum = lax.psum_scatter(
         own_delta.astype(jnp.float32).astype(jnp.bfloat16), "blk", scatter_dimension=0, tiled=True
     )
-    summed = lax.psum(share_sum, ("rep", "sub")).astype(jnp.float32)
+    summed = lax.psum(lax.psum(share_sum, "rep"), "sub").astype(jnp.float32)
     squares = lax.psum(jnp.sum(summed * summed), "blk")
     clip_factor = jnp.minimum(
         jnp.float32(1.0), jnp.sqrt(jnp.float32(entries)) / jnp.sqrt(squares + 1e-06)

time: 87 us -> 98 us (1.13)
  waiting for transfers between devices: 41.9 us -> 53.1 us
    psum x1 -> x2, waiting for transfers between devices: 16.1 us -> 27.2 us  [per_device(): summed = lax.psum(lax.psum(share_sum, 'rep'), 'sub').astype(jnp.float32)]
  transfers between devices with their start and end apart: 2 -> 3, of which waited for: 2 -> 3; matrix products, arithmetic and copies ran while one was open for 0% -> 0% of each run, Pallas kernels for 0% -> 0%
where the time goes in v1:
time: 98 us; the launch traced here: 97.8 us
  waiting for transfers between devices  53.1 us (54%)
  blocking collectives  26.9 us (27%)
  between operations  14.5 us (15%)
  other arithmetic  2.36 us (2%)
    psum x2, waiting for transfers between devices, per_device(): summed = lax.psum(lax.psum(share_sum, 'rep'), 'sub').astype(jnp.float32)  27.2 us
    reduce_scatter x1, waiting for transfers between devices, per_device(): lax.psum_scatter(own_delta.astype(jnp.float32).astype(jnp.bfloat16), 'blk...  25.3 us
    all_gather x1, blocking collectives, per_device(): lax.all_gather(prev_master.astype(jnp.bfloat16), 'blk', axis=0, tiled=True)  14.3 us
    psum x1, blocking collectives, per_device(): squares = lax.psum(jnp.sum(summed * summed), 'blk')  12.7 us
  transfers between devices with their start and end apart: 3, of which 3 were waited for; matrix products, arithmetic and copies ran while one was open for 0% of the time, Pallas kernels for 0%

profile of v1, /device:TPU:0, one launch (start us, length us, event | category | flops | bytes accessed | tf_op | source)
XLA Modules:
  0.0 97.8 jit_solution(17467676497439720712)
XLA Ops:
  7.2 0.0 reduce-scatter.2.cloned.1.call-start
  7.2 0.0 copy-start.1
  7.2 0.7 reduce-scatter.2.cloned.1.call-update
  7.9 0.0 all-reduce.3.cloned.1.call-start
  7.9 25.3 %reduce-scatter.2.cloned.1.call-done = bf16[8,4608]{1,0:T(8,128)(2,1)} async-done(((bf16[32,4608]{1,0:T(8,128)(2,1)}), bf16[8,4608]{1,0:T(8,128)(2,1)}) %reduce-scatter.2.cloned.1.call-update) | async-done | bytes 73744 | tf_op jit(solution)/shard_map/reduce_scatter | solution.py:14
  33.2 0.0 all-reduce.3.cloned.1.call-update
  33.2 0.0 all-reduce.5.cloned.1.call-start
  33.3 0.0 copy-done.1
  33.3 21.3 %all-reduce.3.cloned.1.call-done = bf16[8,4608]{1,0:T(8,128)(2,1)} async-done(((bf16[8,4608]{1,0:T(8,128)(2,1)}), bf16[8,4608]{1,0:T(8,128)(2,1)}) %all-reduce.3.cloned.1.call-update) | async-done | bytes 73744 | tf_op jit(solution)/shard_map/psum | solution.py:17
  54.6 0.0 all-reduce.5.cloned.1.call-update
  54.7 0.0 copy-start.2
  54.7 0.0 copy-start.3
  54.7 14.3 %all_gather.3 = bf16[32,4608]{1,0:T(8,128)(2,1)S(1)} all-gather(bf16[8,4608]{1,0:T(8,128)(2,1)S(1)} %convert_element_type.9), channel_id=1, replica_groups=mesh['groups'=2,'blk'=4,'rep'=2,'sub'=2] {'blk'}, dimensions={0}, use_global_device_ids=true | all-gather | bytes 368640 | tf_op jit(solution)/shard_map/all_gather | solution.py:25
  69.0 5.8 %all-reduce.5.cloned.1.call-done = bf16[8,4608]{1,0:T(8,128)(2,1)} async-done(((bf16[8,4608]{1,0:T(8,128)(2,1)}), bf16[8,4608]{1,0:T(8,128)(2,1)}) %all-reduce.5.cloned.1.call-update) | async-done | bytes 73744 | tf_op jit(solution)/shard_map/psum | solution.py:17
  74.8 0.0 copy-start
  74.8 1.6 %fusion.4 = f32[]{:T(128)} fusion(bf16[8,4608]{1,0:T(8,128)(2,1)} %all-reduce.5.cloned.1.call-done), kind=kLoop, calls=%fused_computation.6 | loop fusion | flops 110591 | bytes 73732 | tf_op jit(solution)/shard_map/reduce_sum | solution.py:18
  76.4 12.7 %psum.23 = f32[]{:T(128)} all-reduce(f32[]{:T(128)} %fusion.4), channel_id=1, replica_groups=mesh['groups'=2,'blk'=4,'rep'=2,'sub'=2] {'blk'}, use_global_device_ids=true, to_apply=%region_4.0 | all-reduce | flops 1 | bytes 8 | tf_op jit(solution)/shard_map/psum | solution.py:18
  89.8 0.0 copy-done.2
  89.8 0.0 copy-done.3
  89.8 0.0 copy-done
  89.8 0.8 fusion.3
  90.5 0.7 copy.10
  (1 shorter events, 0.0 us)
Async XLA Ops:
  7.2 26.0 %reduce-scatter.2.cloned.1.call-start = ((), (), s32[]{:S(2)}) async-start(), calls=%async_computation.1 | async-start | bytes 368640 | tf_op jit(solution)/shard_map/reduce_scatter | solution.py:14
  7.2 26.1 %copy-start.1 = (f32[8,4608]{1,0:T(8,128)S(1)}, f32[8,4608]{1,0:T(8,128)}, u32[]{:S(2)}) copy-start(f32[8,4608]{1,0:T(8,128)} %param.7) | copy-start | bytes 442372
  7.9 46.7 %all-reduce.3.cloned.1.call-start = ((), (), s32[]{:S(2)}) async-start(), calls=%async_computation.2 | async-start | bytes 147456 | tf_op jit(solution)/shard_map/psum | solution.py:17
  33.2 41.6 %all-reduce.5.cloned.1.call-start = ((), (), s32[]{:S(2)}) async-start(), calls=%async_computation.3 | async-start | bytes 147456 | tf_op jit(solution)/shard_map/psum | solution.py:17
  54.7 35.1 %copy-start.2 = (f32[8,4608]{1,0:T(8,128)S(1)}, f32[8,4608]{1,0:T(8,128)}, u32[]{:S(2)}) copy-start(f32[8,4608]{1,0:T(8,128)} %param.6) | copy-start | bytes 442372
  54.7 35.1 %copy-start.3 = (f32[8,4608]{1,0:T(8,128)S(1)}, f32[8,4608]{1,0:T(8,128)}, u32[]{:S(2)}) copy-start(f32[8,4608]{1,0:T(8,128)} %param.5) | copy-start | bytes 442372
  74.8 15.0 %copy-start = (bf16[8,4608]{1,0:T(8,128)(2,1)S(1)}, bf16[8,4608]{1,0:T(8,128)(2,1)}, u32[]{:S(2)}) copy-start(bf16[8,4608]{1,0:T(8,128)(2,1)} %all-reduce.5.cloned.1.call-done) | copy-start | bytes 221188
Sparse Core Ops, SparseCore 0:
  10.2 22.9 reduce-scatter.1
  35.4 19.1 all-reduce.2
  56.9 17.8 all-reduce.4

commit v2 on v0

--- a/solution.py
+++ b/solution.py
@@ -14,7 +14,7 @@
     share_sum = lax.psum_scatter(
         own_delta.astype(jnp.float32).astype(jnp.bfloat16), "blk", scatter_dimension=0, tiled=True
     )
-    summed = lax.psum(share_sum, ("rep", "sub")).astype(jnp.float32)
+    summed = jnp.sum(lax.all_gather(share_sum, ("rep", "sub")), axis=0).astype(jnp.float32)
     squares = lax.psum(jnp.sum(summed * summed), "blk")
     clip_factor = jnp.minimum(
         jnp.float32(1.0), jnp.sqrt(jnp.float32(entries)) / jnp.sqrt(squares + 1e-06)

time: 87 us -> 59.3 us (0.68)
  waiting for transfers between devices: 41.9 us -> 9.47 us
  blocking collectives: 26.8 us -> 32.4 us
  other arithmetic: 2.36 us -> 1.44 us
    reduce_scatter x1, waiting for transfers between devices: 25.1 us -> 8.8 us  [per_device(): lax.psum_scatter(own_delta.astype(jnp.float32).astype(jnp.bfloat16), 'blk...]
    psum x1 -> x0, waiting for transfers between devices: 16.1 us -> none  [per_device(): summed = lax.psum(share_sum, ('rep', 'sub')).astype(jnp.float32)]
    all_gather x0 -> x1, blocking collectives: none -> 6.08 us  [per_device(): lax.all_gather(share_sum, ('rep', 'sub'))]
    psum x1, blocking collectives: 12.7 us -> 9.52 us  [per_device(): squares = lax.psum(jnp.sum(summed * summed), 'blk')]
    all_gather x1, blocking collectives: 14.1 us -> 16.8 us  [per_device(): lax.all_gather(prev_master.astype(jnp.bfloat16), 'blk', axis=0, tiled=True)]
    reduce_sum x1, other arithmetic: 1.6 us -> 0.64 us  [per_device(): squares = lax.psum(jnp.sum(summed * summed), 'blk')]
  transfers between devices with their start and end apart: 2 -> 1, of which waited for: 2 -> 1; matrix products, arithmetic and copies ran while one was open for 0% -> 0% of each run, Pallas kernels for 0% -> 0%
where the time goes in v2:
time: 59.3 us; the launch traced here: 59.1 us
  blocking collectives  32.4 us (55%)
  between operations  14.8 us (25%)
  waiting for transfers between devices  9.47 us (16%)
  other arithmetic  1.44 us (2%)
  local copies, waits for them, and re-layouts  0.95 us (2%)
    all_gather x1, blocking collectives, per_device(): lax.all_gather(prev_master.astype(jnp.bfloat16), 'blk', axis=0, tiled=True)  16.8 us
    psum x1, blocking collectives, per_device(): squares = lax.psum(jnp.sum(summed * summed), 'blk')  9.52 us
    reduce_scatter x1, waiting for transfers between devices, per_device(): lax.psum_scatter(own_delta.astype(jnp.float32).astype(jnp.bfloat16), 'blk...  8.8 us
    all_gather x1, blocking collectives, per_device(): lax.all_gather(share_sum, ('rep', 'sub'))  6.08 us
  transfers between devices with their start and end apart: 1, of which 1 were waited for; matrix products, arithmetic and copies ran while one was open for 0% of the time, Pallas kernels for 0%

profile of v2, /device:TPU:0, one launch (start us, length us, event | category | flops | bytes accessed | tf_op | source)
XLA Modules:
  0.0 59.1 jit_solution(8711837118970726585)
XLA Ops:
  7.2 0.0 reduce-scatter.2.cloned.1.call-start
  7.2 0.0 copy-start
  7.2 0.7 %reduce-scatter.2.cloned.1.call-update = ((bf16[32,4608]{1,0:T(8,128)(2,1)}), bf16[8,4608]{1,0:T(8,128)(2,1)}) async-update(((), (), s32[]{:S(2)}) %reduce-scatter.2.cloned.1.call-start, bf16[32,4608]{1,0:T(8,128)(2,1)} %bitcast.3) | async-update | bytes 663576
  7.9 0.2 copy-done
  8.1 16.8 %all_gather.11 = bf16[32,4608]{1,0:T(8,128)(2,1)S(1)} all-gather(bf16[8,4608]{1,0:T(8,128)(2,1)S(1)} %convert_element_type.5), channel_id=1, replica_groups=mesh['groups'=2,'blk'=4,'rep'=2,'sub'=2] {'blk'}, dimensions={0}, use_global_device_ids=true | all-gather | bytes 368640 | tf_op jit(solution)/shard_map/all_gather | solution.py:25
  25.0 8.8 %reduce-scatter.2.cloned.1.call-done = bf16[8,4608]{1,0:T(8,128)(2,1)} async-done(((bf16[32,4608]{1,0:T(8,128)(2,1)}), bf16[8,4608]{1,0:T(8,128)(2,1)}) %reduce-scatter.2.cloned.1.call-update) | async-done | bytes 73744 | tf_op jit(solution)/shard_map/reduce_scatter | solution.py:14
  33.8 6.1 %all-gather = bf16[32,4608]{1,0:T(8,128)(2,1)S(1)} all-gather(bf16[8,4608]{1,0:T(8,128)(2,1)} %reduce-scatter.2.cloned.1.call-done), channel_id=2, replica_groups=mesh['groups'=2,'blk'=4,'rep'=2,'sub'=2] {'rep','sub'}, dimensions={0}, use_global_device_ids=true | all-gather | bytes 368640 | tf_op jit(solution)/shard_map/all_gather | solution.py:17
  39.8 0.0 copy-start.1
  39.8 0.0 copy-start.2
  39.9 0.6 %fusion.4 = f32[]{:T(128)} fusion(bf16[8,4608]{1,0:T(8,128)(2,1)S(1)} %bitcast_reduce_fusion), kind=kLoop, calls=%fused_computation.7 | loop fusion | flops 110591 | bytes 73732 | tf_op jit(solution)/shard_map/reduce_sum | solution.py:18
  40.5 9.5 %psum.7 = f32[]{:T(128)} all-reduce(f32[]{:T(128)} %fusion.4), channel_id=1, replica_groups=mesh['groups'=2,'blk'=4,'rep'=2,'sub'=2] {'blk'}, use_global_device_ids=true, to_apply=%region_3.0 | all-reduce | flops 1 | bytes 8 | tf_op jit(solution)/shard_map/psum | solution.py:18
  50.7 0.0 copy-done.1
  50.8 0.0 copy-done.2
  50.8 0.8 %fusion.3 = (f32[8,4608]{1,0:T(8,128)}, f32[8,4608]{1,0:T(8,128)}) fusion(f32[8,4608]{1,0:T(8,128)S(1)} %copy-done.1, bf16[8,4608]{1,0:T(8,128)(2,1)S(1)} %bitcast_reduce_fusion, f32[]{:T(128)S(6)} %min_shard_map.3, f32[8,4608]{1,0:T(8,128)S(1)} %copy-done.2), kind=kLoop, calls=%fused_computation.6 | loop fusion | flops 294912 | bytes 663556 | tf_op jit(solution)/shard_map/sub | solution.py:24
  51.5 0.7 %copy.8 = bf16[32,4608]{1,0:T(8,128)(2,1)} copy(bf16[32,4608]{1,0:T(8,128)(2,1)S(1)} %all_gather.11) | data formatting | bytes 589824
  (2 shorter events, 0.0 us)
Async XLA Ops:
  7.2 26.6 %reduce-scatter.2.cloned.1.call-start = ((), (), s32[]{:S(2)}) async-start(), calls=%async_computation.1 | async-start | bytes 368640 | tf_op jit(solution)/shard_map/reduce_scatter | solution.py:14
  7.2 0.9 %copy-start = (f32[8,4608]{1,0:T(8,128)S(1)}, f32[8,4608]{1,0:T(8,128)}, u32[]{:S(2)}) copy-start(f32[8,4608]{1,0:T(8,128)} %param.7) | copy-start | bytes 442372
  39.8 10.9 %copy-start.1 = (f32[8,4608]{1,0:T(8,128)S(1)}, f32[8,4608]{1,0:T(8,128)}, u32[]{:S(2)}) copy-start(f32[8,4608]{1,0:T(8,128)} %param.6) | copy-start | bytes 442372
  39.8 10.9 %copy-start.2 = (f32[8,4608]{1,0:T(8,128)S(1)}, f32[8,4608]{1,0:T(8,128)}, u32[]{:S(2)}) copy-start(f32[8,4608]{1,0:T(8,128)} %param.5) | copy-start | bytes 442372
Sparse Core Ops, SparseCore 0:
  10.2 23.4 reduce-scatter.1
